TPU v7x, 32 devices: a whole 2x2x4 slice. The times are simulated.
32 devices in a mesh: section: 16 (over z, x, core), dp: 2 (over y).
Axes of the slice: x: 2, y: 2, z: 4, core: 2. Of those that a mesh axis runs over, the one named last changes fastest.
Arguments:
- cotangent: bfloat16 [128, 8192], P('dp'), may hold values from -96 to 96
- lengths: int32 [4], P('dp'), may hold values from 1 to 32, as said below
- example_ids: int32 [128], P('dp'), may hold values from -1 to 3, as said below
- layer_inputs: bfloat16 [128, 32768], P('dp', 'section'), may hold values from -6 to 6
- preacts: bfloat16 [128, 32768], P('dp', 'section'), may hold values from -6 to 6
- weights: bfloat16 [32768, 8192], P('section', 'dp'), may hold values from -0.0625 to 0.0625
- query_left: bfloat16 [32768, 256], P('section'), may hold values from -0.0625 to 0.0625
- query_right: bfloat16 [32768, 256], P('section'), may hold values from -0.0625 to 0.0625
Outputs:
- input_grads: bfloat16 [128, 32768], P('dp', 'section')
- scores: float32 [4, 16], P('dp')
Inputs may be any that keep to these rules, and one draw needn't show every extreme that they name: In each aligned block of 2 sequences one length is exactly 32; the lengths of a block sum to at most 64. `example_ids`: rows n * 64 to (n + 1) * 64 - 1 hold sequences n * 2 to (n + 1) * 2 - 1 in order from the block's first row, each on as many consecutive rows as its length; the block's remaining rows hold -1.
All inputs are finite; a program needn't handle non-finite values.
Results may differ from a plain program's by a relative error of at most 0.0066.
Values may be sent and summed in bfloat16 or wider, within the bound.
No kernel may reach another device: no remote copies, remote signals or barrier semaphores. Data moves between devices by JAX's collectives and lax.ppermute only.
A program may use at most 64 MiB of HBM per device.

v0:
```python
import jax
import jax.numpy as jnp
from jax import lax
from jax.sharding import PartitionSpec as P

LAYERS = 4
QUERIES = 16
RANK = 16
ROWS = 32


def from_partner(value, axis, distance):
    mask = 2**distance
    pairs = [(source, source ^ mask) for source in range(lax.axis_size(axis))]
    return lax.ppermute(value, axis, pairs)


def from_behind(value, axis, steps):
    count = lax.axis_size(axis)
    first, last = (max(0, -steps), min(count, count - steps))
    return lax.ppermute(value, axis, [(source, source + steps) for source in range(first, last)])


def silu_slope(preact):
    sigmoid_value = jax.nn.sigmoid(preact)
    return sigmoid_value * (1.0 + preact * (1.0 - sigmoid_value))


def per_device(
    cotangent, lengths, example_ids, layer_inputs, preacts, weights, query_left, query_right
):
    per_section = lax.axis_size("section") // LAYERS
    level_count = per_section.bit_length() - 1
    position = lax.axis_index("section")
    section_index = position // per_section
    column_block = position % per_section
    group_index = lax.axis_index("dp")
    token_count = cotangent.shape[0]
    block_cols = layer_inputs.shape[1]
    seq_count = lengths.shape[0]
    micro_count = token_count // ROWS
    step_count = LAYERS + micro_count - 1
    seq_slots = group_index * seq_count + jnp.arange(seq_count, dtype=jnp.int32)
    member = (example_ids[:, None] == seq_slots[None, :]).astype(jnp.float32)
    token_len = jnp.dot(member, lengths.astype(jnp.float32), precision=lax.Precision.HIGHEST)
    token_scale = jnp.where(example_ids >= 0, 1.0 / jnp.maximum(token_len, 1.0), 0.0)
    top_columns = lax.dynamic_slice_in_dim(cotangent, column_block * block_cols, block_cols, 1)
    top_grad = (top_columns.astype(jnp.float32) * token_scale[:, None]).astype(jnp.bfloat16)
    right_full = query_right
    for level_bit in range(level_count):
        partner = from_partner(right_full, "section", level_bit)
        upper_half = column_block >> level_bit & 1
        right_full = jnp.where(
            upper_half == 1,
            jnp.concatenate([partner, right_full], 0),
            jnp.concatenate([right_full, partner], 0),
        )

    def gather_gate(gate_grad):
        combined = gate_grad
        for level_bit in range(level_count):
            partner = from_partner(combined, "section", level_bit)
            upper_half = column_block >> level_bit & 1
            combined = jnp.where(
                upper_half == 1,
                jnp.concatenate([partner, combined], 1),
                jnp.concatenate([combined, partner], 1),
            )
        return combined

    def score_terms(gate_full, input_rows, id_rows):
        left_part = jnp.dot(input_rows, query_left, preferred_element_type=jnp.float32)
        right_part = jnp.dot(gate_full, right_full, preferred_element_type=jnp.float32)
        per_token = jnp.sum((left_part * right_part).reshape(ROWS, QUERIES, RANK), axis=2)
        block_member = (id_rows[:, None] == seq_slots[None, :]).astype(jnp.float32)
        return jnp.dot(block_member.T, per_token, precision=lax.Precision.HIGHEST)

    def advance(clock_tick, loop_state):
        outgoing, grad_store, totals = loop_state
        arrived = from_behind(outgoing, "section", -per_section)
        micro_index = clock_tick - (LAYERS - 1 - section_index)
        in_range = (micro_index >= 0) & (micro_index < micro_count)
        row_start = jnp.clip(micro_index, 0, micro_count - 1) * ROWS
        top_rows = lax.dynamic_slice_in_dim(top_grad, row_start, ROWS, 0)
        grad_out = jnp.where(section_index == LAYERS - 1, top_rows, arrived)
        preact = lax.dynamic_slice_in_dim(preacts, row_start, ROWS, 0).astype(jnp.float32)
        gate_grad = (silu_slope(preact) * grad_out.astype(jnp.float32)).astype(jnp.bfloat16)
        gate_full = gather_gate(gate_grad)
        input_rows = lax.dynamic_slice_in_dim(layer_inputs, row_start, ROWS, 0)
        id_rows = lax.dynamic_slice_in_dim(example_ids, row_start, ROWS, 0)
        by_group = lax.all_to_all(gate_full, "dp", split_axis=1, concat_axis=0, tiled=True)
        backward_sum = lax.psum_scatter(
            lax.dot_general(
                by_group, weights, (((1,), (1,)), ((), ())), preferred_element_type=jnp.float32
            ),
            "dp",
            scatter_dimension=0,
            tiled=True,
        )
        increment = score_terms(gate_full, input_rows, id_rows)
        in_grad = (grad_out.astype(jnp.float32) + backward_sum).astype(jnp.bfloat16)
        updated = lax.dynamic_update_slice_in_dim(grad_store, in_grad, row_start, 0)
        grad_store = jnp.where(in_range, updated, grad_store)
        increment = jnp.where(in_range, increment, 0.0)
        totals = totals + lax.psum(increment, "section")
        return (in_grad, grad_store, totals)

    initial = (
        jnp.zeros((ROWS, block_cols), jnp.bfloat16),
        jnp.zeros((token_count, block_cols), jnp.bfloat16),
        jnp.zeros((seq_count, QUERIES), jnp.float32),
    )
    outgoing, grad_store, totals = lax.fori_loop(0, step_count, advance, initial)
    return (grad_store, totals)


def solution(mesh):
    placed = (
        P("dp", None),
        P("dp"),
        P("dp"),
        P("dp", "section"),
        P("dp", "section"),
        P("section", "dp"),
        P("section", None),
        P("section", None),
    )
    return jax.shard_map(
        per_device,
        mesh=mesh,
        in_specs=placed,
        out_specs=(P("dp", "section"), P("dp", None)),
        check_vma=False,
    )
```

profile of v0, /device:TPU:0, one launch (start us, length us, event | category | flops | bytes accessed | tf_op | source)
XLA Modules:
  0.0 443.8 jit_solution(1843948315144772857)
XLA Ops:
  7.2 0.6 collective-permute-start.3
  7.7 2.5 collective-permute-done.3
  10.2 3.4 maximum_select_fusion.6
  13.6 2.8 collective-permute-start.4
  16.6 1.1 multiply_convert_fusion
  17.8 44.9 %collective-permute-done.4 = bf16[4096,256]{1,0:T(8,128)(2,1)} collective-permute-done((bf16[4096,256]{1,0:T(8,128)(2,1)}, bf16[4096,256]{1,0:T(8,128)(2,1)}, u32[]{:S(2)}, u32[]{:S(2)}) %collective-permute-start.4) | collective-permute-done | bytes 2097184 | tf_op jit(solution)/shard_map/ppermute | solution.py:15
  62.7 5.5 %maximum_select_fusion.5 = bf16[8192,256]{1,0:T(8,128)(2,1)} fusion(bf16[4096,256]{1,0:T(8,128)(2,1)} %maximum_select_fusion.6, bf16[4096,256]{1,0:T(8,128)(2,1)} %collective-permute-done.4, pred[]{:T(512)} %eq.87), kind=kLoop, calls=%fused_computation.37 | loop fusion | flops 18874368 | bytes 8388609 | tf_op jit(solution)/shard_map/jit(_where)/select_n | solution.py:53
  68.3 368.3 %while.20 = (s32[]{:T(128)}, bf16[32,2048]{1,0:T(8,128)(2,1)S(1)}, bf16[64,2048]{1,0:T(8,128)(2,1)S(1)}, f32[2,16]{1,0:T(2,128)S(1)}, pred[]{:T(512)}, /*index=5...) while((s32[]{:T(128)}, bf16[32,2048]{1,0:T(8,128)(2,1)S(1)}, ...), condition=%wide.region_4.5_spmd.clone, body=%wide.region_0.4_spmd.clone.sunk | while | flops 1248227072 | bytes 33232504 | solution.py:113
  68.4 1.3 collective-permute-start
  69.7 5.5 %collective-permute-done = bf16[32,2048]{1,0:T(8,128)(2,1)S(1)} collective-permute-done((bf16[32,2048]{1,0:T(8,128)(2,1)S(1)}, bf16[32,2048]{1,0:T(8,128)(2,1)S(1)}, u32[]{:S(2)}, u32[]{:S(2)}) %collective-permute-start) | collective-permute-done | bytes 131104 | tf_op jit(solution)/shard_map/while/body/eval_jaxpr/ppermute | solution.py:21
  75.4 1.3 collective-permute-done.1
  76.8 1.8 collective-permute-start.2
  78.7 6.5 %collective-permute-done.2 = bf16[32,4096]{1,0:T(8,128)(2,1)S(1)} collective-permute-done((bf16[32,4096]{1,0:T(8,128)(2,1)S(1)}, bf16[32,4096]{1,0:T(8,128)(2,1)S(1)}, u32[]{:S(2)}, u32[]{:S(2)}) %collective-permute-start.2) | collective-permute-done | bytes 262176 | tf_op jit(solution)/shard_map/while/body/eval_jaxpr/ppermute | solution.py:15
  85.3 10.3 %all_to_all.38 = bf16[32,2,4096]{2,0,1:T(8,128)(2,1)S(1)} all-to-all(bf16[32,2,4096]{2,0,1:T(8,128)(2,1)S(1)} %maximum_select_fusion.14), channel_id=1, replica_groups=mesh['section'=16,'dp'=2] {'dp'}, dimensions={1} | all-to-all | bytes 1048576 | tf_op jit(solution)/shard_map/while/body/eval_jaxpr/all_to_all | solution.py:91
  95.6 11.8 %fusion.50 = f32[64,2048]{1,0:T(8,128)} fusion(bf16[64,4096]{1,0:T(8,128)(2,1)S(1)} %bitcast.44, bf16[2048,4096]{1,0:T(8,128)(2,1)} %get-tuple-element.579), kind=kOutput, calls=%fused_computation.49.clone.1 | convolution fusion | flops 1073741824 | bytes 17825792 | tf_op jit(solution)/shard_map/while/body/eval_jaxpr/dot_general | solution.py:93
  107.4 0.3 fusion.51
  107.8 2.9 convolution_multiply_fusion.2
  110.8 0.3 convolution_select_fusion.2
  111.1 30.1 %psum.15 = f32[2,16]{1,0:T(2,128)S(1)} all-reduce(f32[2,16]{1,0:T(2,128)S(1)} %convolution_select_fusion.2), channel_id=1, replica_groups=mesh['section'=16,'dp'=2] {'section'}, use_global_device_ids=true, to_apply=%region_3.3 | all-reduce | flops 32 | bytes 256 | tf_op jit(solution)/shard_map/while/body/eval_jaxpr/psum | solution.py:105
  141.2 1.0 select_dynamic-update-slice_fusion.2
  142.3 1.3 collective-permute-start
  143.6 5.5 %collective-permute-done = bf16[32,2048]{1,0:T(8,128)(2,1)S(1)} collective-permute-done((bf16[32,2048]{1,0:T(8,128)(2,1)S(1)}, bf16[32,2048]{1,0:T(8,128)(2,1)S(1)}, u32[]{:S(2)}, u32[]{:S(2)}) %collective-permute-start) | collective-permute-done | bytes 131104 | tf_op jit(solution)/shard_map/while/body/eval_jaxpr/ppermute | solution.py:21
  149.4 1.3 collective-permute-done.1
  151.0 8.3 %collective-permute-done.2 = bf16[32,4096]{1,0:T(8,128)(2,1)S(1)} collective-permute-done((bf16[32,4096]{1,0:T(8,128)(2,1)S(1)}, bf16[32,4096]{1,0:T(8,128)(2,1)S(1)}, u32[]{:S(2)}, u32[]{:S(2)}) %collective-permute-start.2) | collective-permute-done | bytes 262176 | tf_op jit(solution)/shard_map/while/body/eval_jaxpr/ppermute | solution.py:15
  159.3 10.1 %all_to_all.38 = bf16[32,2,4096]{2,0,1:T(8,128)(2,1)S(1)} all-to-all(bf16[32,2,4096]{2,0,1:T(8,128)(2,1)S(1)} %maximum_select_fusion.14), channel_id=1, replica_groups=mesh['section'=16,'dp'=2] {'dp'}, dimensions={1} | all-to-all | bytes 1048576 | tf_op jit(solution)/shard_map/while/body/eval_jaxpr/all_to_all | solution.py:91
  169.4 11.8 %fusion.50 = f32[64,2048]{1,0:T(8,128)} fusion(bf16[64,4096]{1,0:T(8,128)(2,1)S(1)} %bitcast.44, bf16[2048,4096]{1,0:T(8,128)(2,1)} %get-tuple-element.579), kind=kOutput, calls=%fused_computation.49.clone.1 | convolution fusion | flops 1073741824 | bytes 17825792 | tf_op jit(solution)/shard_map/while/body/eval_jaxpr/dot_general | solution.py:93
  181.2 0.3 fusion.51
  181.6 3.0 convolution_multiply_fusion.2
  184.7 0.3 convolution_select_fusion.2
  185.0 29.5 %psum.15 = f32[2,16]{1,0:T(2,128)S(1)} all-reduce(f32[2,16]{1,0:T(2,128)S(1)} %convolution_select_fusion.2), channel_id=1, replica_groups=mesh['section'=16,'dp'=2] {'section'}, use_global_device_ids=true, to_apply=%region_3.3 | all-reduce | flops 32 | bytes 256 | tf_op jit(solution)/shard_map/while/body/eval_jaxpr/psum | solution.py:105
  214.5 1.0 select_dynamic-update-slice_fusion.2
  215.6 1.3 collective-permute-start
  216.9 5.9 %collective-permute-done = bf16[32,2048]{1,0:T(8,128)(2,1)S(1)} collective-permute-done((bf16[32,2048]{1,0:T(8,128)(2,1)S(1)}, bf16[32,2048]{1,0:T(8,128)(2,1)S(1)}, u32[]{:S(2)}, u32[]{:S(2)}) %collective-permute-start) | collective-permute-done | bytes 131104 | tf_op jit(solution)/shard_map/while/body/eval_jaxpr/ppermute | solution.py:21
  223.1 1.3 collective-permute-done.1
  224.6 8.3 %collective-permute-done.2 = bf16[32,4096]{1,0:T(8,128)(2,1)S(1)} collective-permute-done((bf16[32,4096]{1,0:T(8,128)(2,1)S(1)}, bf16[32,4096]{1,0:T(8,128)(2,1)S(1)}, u32[]{:S(2)}, u32[]{:S(2)}) %collective-permute-start.2) | collective-permute-done | bytes 262176 | tf_op jit(solution)/shard_map/while/body/eval_jaxpr/ppermute | solution.py:15
  233.0 10.1 %all_to_all.38 = bf16[32,2,4096]{2,0,1:T(8,128)(2,1)S(1)} all-to-all(bf16[32,2,4096]{2,0,1:T(8,128)(2,1)S(1)} %maximum_select_fusion.14), channel_id=1, replica_groups=mesh['section'=16,'dp'=2] {'dp'}, dimensions={1} | all-to-all | bytes 1048576 | tf_op jit(solution)/shard_map/while/body/eval_jaxpr/all_to_all | solution.py:91
  243.1 11.8 %fusion.50 = f32[64,2048]{1,0:T(8,128)} fusion(bf16[64,4096]{1,0:T(8,128)(2,1)S(1)} %bitcast.44, bf16[2048,4096]{1,0:T(8,128)(2,1)} %get-tuple-element.579), kind=kOutput, calls=%fused_computation.49.clone.1 | convolution fusion | flops 1073741824 | bytes 17825792 | tf_op jit(solution)/shard_map/while/body/eval_jaxpr/dot_general | solution.py:93
  254.9 0.3 fusion.51
  255.3 3.0 convolution_multiply_fusion.2
  258.4 0.3 convolution_select_fusion.2
  258.7 29.5 %psum.15 = f32[2,16]{1,0:T(2,128)S(1)} all-reduce(f32[2,16]{1,0:T(2,128)S(1)} %convolution_select_fusion.2), channel_id=1, replica_groups=mesh['section'=16,'dp'=2] {'section'}, use_global_device_ids=true, to_apply=%region_3.3 | all-reduce | flops 32 | bytes 256 | tf_op jit(solution)/shard_map/while/body/eval_jaxpr/psum | solution.py:105
  288.2 1.0 select_dynamic-update-slice_fusion.2
  289.3 1.3 collective-permute-start
  290.6 5.9 %collective-permute-done = bf16[32,2048]{1,0:T(8,128)(2,1)S(1)} collective-permute-done((bf16[32,2048]{1,0:T(8,128)(2,1)S(1)}, bf16[32,2048]{1,0:T(8,128)(2,1)S(1)}, u32[]{:S(2)}, u32[]{:S(2)}) %collective-permute-start) | collective-permute-done | bytes 131104 | tf_op jit(solution)/shard_map/while/body/eval_jaxpr/ppermute | solution.py:21
  296.8 1.3 collective-permute-done.1
  298.3 8.3 %collective-permute-done.2 = bf16[32,4096]{1,0:T(8,128)(2,1)S(1)} collective-permute-done((bf16[32,4096]{1,0:T(8,128)(2,1)S(1)}, bf16[32,4096]{1,0:T(8,128)(2,1)S(1)}, u32[]{:S(2)}, u32[]{:S(2)}) %collective-permute-start.2) | collective-permute-done | bytes 262176 | tf_op jit(solution)/shard_map/while/body/eval_jaxpr/ppermute | solution.py:15
  306.7 10.1 %all_to_all.38 = bf16[32,2,4096]{2,0,1:T(8,128)(2,1)S(1)} all-to-all(bf16[32,2,4096]{2,0,1:T(8,128)(2,1)S(1)} %maximum_select_fusion.14), channel_id=1, replica_groups=mesh['section'=16,'dp'=2] {'dp'}, dimensions={1} | all-to-all | bytes 1048576 | tf_op jit(solution)/shard_map/while/body/eval_jaxpr/all_to_all | solution.py:91
  316.8 11.8 %fusion.50 = f32[64,2048]{1,0:T(8,128)} fusion(bf16[64,4096]{1,0:T(8,128)(2,1)S(1)} %bitcast.44, bf16[2048,4096]{1,0:T(8,128)(2,1)} %get-tuple-element.579), kind=kOutput, calls=%fused_computation.49.clone.1 | convolution fusion | flops 1073741824 | bytes 17825792 | tf_op jit(solution)/shard_map/while/body/eval_jaxpr/dot_general | solution.py:93
  328.6 0.3 fusion.51
  329.0 3.0 convolution_multiply_fusion.2
  332.1 0.3 convolution_select_fusion.2
  332.4 29.5 %psum.15 = f32[2,16]{1,0:T(2,128)S(1)} all-reduce(f32[2,16]{1,0:T(2,128)S(1)} %convolution_select_fusion.2), channel_id=1, replica_groups=mesh['section'=16,'dp'=2] {'section'}, use_global_device_ids=true, to_apply=%region_3.3 | all-reduce | flops 32 | bytes 256 | tf_op jit(solution)/shard_map/while/body/eval_jaxpr/psum | solution.py:105
  361.9 1.0 select_dynamic-update-slice_fusion.2
  363.0 1.3 collective-permute-start
  364.3 5.9 %collective-permute-done = bf16[32,2048]{1,0:T(8,128)(2,1)S(1)} collective-permute-done((bf16[32,2048]{1,0:T(8,128)(2,1)S(1)}, bf16[32,2048]{1,0:T(8,128)(2,1)S(1)}, u32[]{:S(2)}, u32[]{:S(2)}) %collective-permute-start) | collective-permute-done | bytes 131104 | tf_op jit(solution)/shard_map/while/body/eval_jaxpr/ppermute | solution.py:21
  370.5 1.3 collective-permute-done.1
  372.0 8.3 %collective-permute-done.2 = bf16[32,4096]{1,0:T(8,128)(2,1)S(1)} collective-permute-done((bf16[32,4096]{1,0:T(8,128)(2,1)S(1)}, bf16[32,4096]{1,0:T(8,128)(2,1)S(1)}, u32[]{:S(2)}, u32[]{:S(2)}) %collective-permute-start.2) | collective-permute-done | bytes 262176 | tf_op jit(solution)/shard_map/while/body/eval_jaxpr/ppermute | solution.py:15
  380.4 10.1 %all_to_all.38 = bf16[32,2,4096]{2,0,1:T(8,128)(2,1)S(1)} all-to-all(bf16[32,2,4096]{2,0,1:T(8,128)(2,1)S(1)} %maximum_select_fusion.14), channel_id=1, replica_groups=mesh['section'=16,'dp'=2] {'dp'}, dimensions={1} | all-to-all | bytes 1048576 | tf_op jit(solution)/shard_map/while/body/eval_jaxpr/all_to_all | solution.py:91
  390.5 11.8 %fusion.50 = f32[64,2048]{1,0:T(8,128)} fusion(bf16[64,4096]{1,0:T(8,128)(2,1)S(1)} %bitcast.44, bf16[2048,4096]{1,0:T(8,128)(2,1)} %get-tuple-element.579), kind=kOutput, calls=%fused_computation.49.clone.1 | convolution fusion | flops 1073741824 | bytes 17825792 | tf_op jit(solution)/shard_map/while/body/eval_jaxpr/dot_general | solution.py:93
  402.3 0.3 fusion.51
  402.7 3.0 convolution_multiply_fusion.2
  406.0 29.5 %psum.15 = f32[2,16]{1,0:T(2,128)S(1)} all-reduce(f32[2,16]{1,0:T(2,128)S(1)} %convolution_select_fusion.2), channel_id=1, replica_groups=mesh['section'=16,'dp'=2] {'section'}, use_global_device_ids=true, to_apply=%region_3.3 | all-reduce | flops 32 | bytes 256 | tf_op jit(solution)/shard_map/while/body/eval_jaxpr/psum | solution.py:105
  435.6 1.0 select_dynamic-update-slice_fusion.2
  436.6 0.7 copy-done.1
  (93 shorter events, 4.4 us)
Async XLA Ops:
  7.2 9.3 %copy-start.5 = (s32[2]{0:T(128)S(1)}, s32[2]{0:T(128)}, u32[]{:S(2)}) copy-start(s32[2]{0:T(128)} %param.11) | copy-start | bytes 28
  7.2 9.3 %copy-start.6 = (s32[64]{0:T(128)S(1)}, s32[64]{0:T(128)}, u32[]{:S(2)}) copy-start(s32[64]{0:T(128)} %param.12) | copy-start | bytes 772
  7.2 3.1 collective-permute-start.3
  13.6 49.1 %collective-permute-start.4 = (bf16[4096,256]{1,0:T(8,128)(2,1)}, bf16[4096,256]{1,0:T(8,128)(2,1)}, u32[]{:S(2)}, u32[]{:S(2)}) collective-permute-start(bf16[4096,256]{1,0:T(8,128)(2,1)} %maximum_select_fusion.6), channel_id=1, source_target_pairs={{0,4},{2,6},{4,0},{6,2},{8,12},{10,14},{12,8},{14,10},{16,20},{18,... | collective-permute-start | bytes 6291464 | tf_op jit(solution)/shard_map/ppermute | solution.py:15
  17.8 50.5 %copy-start = (bf16[2048,256]{1,0:T(8,128)(2,1)S(1)}, bf16[2048,256]{1,0:T(8,128)(2,1)}, u32[]{:S(2)}) copy-start(bf16[2048,256]{1,0:T(8,128)(2,1)} %param.16) | copy-start | bytes 3145732
  17.8 50.5 %copy-start.2 = (bf16[64,2048]{1,0:T(8,128)(2,1)S(1)}, bf16[64,2048]{1,0:T(8,128)(2,1)}, u32[]{:S(2)}) copy-start(bf16[64,2048]{1,0:T(8,128)(2,1)} %param.13) | copy-start | bytes 786436
  17.8 50.5 %copy-start.3 = (bf16[64,2048]{1,0:T(8,128)(2,1)S(1)}, bf16[64,2048]{1,0:T(8,128)(2,1)}, u32[]{:S(2)}) copy-start(bf16[64,2048]{1,0:T(8,128)(2,1)} %param.14) | copy-start | bytes 786436
  68.3 72.9 %reduce-scatter.2.cloned.1.call-start = ((), (), s32[]{:S(2)}) async-start(), calls=%async_computation.2 | async-start | bytes 786432 | tf_op jit(solution)/shard_map/while/body/eval_jaxpr/reduce_scatter | solution.py:92
  68.4 6.9 %collective-permute-start = (bf16[32,2048]{1,0:T(8,128)(2,1)S(1)}, bf16[32,2048]{1,0:T(8,128)(2,1)S(1)}, u32[]{:S(2)}, u32[]{:S(2)}) collective-permute-start(bf16[32,2048]{1,0:T(8,128)(2,1)S(1)} %broadcast_select_fusion.2), channel_id=1, source_target_pairs={{8,0},{10,2},{12,4},{14,6},{16,8},{18,10},{20,12},{22,14},{24,16},... | collective-permute-start | bytes 393224 | tf_op jit(solution)/shard_map/while/body/eval_jaxpr/ppermute | solution.py:21
  75.3 1.4 collective-permute-start.1
  76.8 8.4 %collective-permute-start.2 = (bf16[32,4096]{1,0:T(8,128)(2,1)S(1)}, bf16[32,4096]{1,0:T(8,128)(2,1)S(1)}, u32[]{:S(2)}, u32[]{:S(2)}) collective-permute-start(bf16[32,4096]{1,0:T(8,128)(2,1)S(1)} %maximum_select_fusion.13), channel_id=1, source_target_pairs={{0,4},{2,6},{4,0},{6,2},{8,12},{10,14},{12,8},{14,10},{16,20},{18,... | collective-permute-start | bytes 786440 | tf_op jit(solution)/shard_map/while/body/eval_jaxpr/ppermute | solution.py:15
  142.2 72.2 %reduce-scatter.2.cloned.1.call-start = ((), (), s32[]{:S(2)}) async-start(), calls=%async_computation.2 | async-start | bytes 786432 | tf_op jit(solution)/shard_map/while/body/eval_jaxpr/reduce_scatter | solution.py:92
  142.3 6.9 %collective-permute-start = (bf16[32,2048]{1,0:T(8,128)(2,1)S(1)}, bf16[32,2048]{1,0:T(8,128)(2,1)S(1)}, u32[]{:S(2)}, u32[]{:S(2)}) collective-permute-start(bf16[32,2048]{1,0:T(8,128)(2,1)S(1)} %broadcast_select_fusion.2), channel_id=1, source_target_pairs={{8,0},{10,2},{12,4},{14,6},{16,8},{18,10},{20,12},{22,14},{24,16},... | collective-permute-start | bytes 393224 | tf_op jit(solution)/shard_map/while/body/eval_jaxpr/ppermute | solution.py:21
  149.3 1.4 collective-permute-start.1
  150.8 8.4 %collective-permute-start.2 = (bf16[32,4096]{1,0:T(8,128)(2,1)S(1)}, bf16[32,4096]{1,0:T(8,128)(2,1)S(1)}, u32[]{:S(2)}, u32[]{:S(2)}) collective-permute-start(bf16[32,4096]{1,0:T(8,128)(2,1)S(1)} %maximum_select_fusion.13), channel_id=1, source_target_pairs={{0,4},{2,6},{4,0},{6,2},{8,12},{10,14},{12,8},{14,10},{16,20},{18,... | collective-permute-start | bytes 786440 | tf_op jit(solution)/shard_map/while/body/eval_jaxpr/ppermute | solution.py:15
  215.5 72.6 %reduce-scatter.2.cloned.1.call-start = ((), (), s32[]{:S(2)}) async-start(), calls=%async_computation.2 | async-start | bytes 786432 | tf_op jit(solution)/shard_map/while/body/eval_jaxpr/reduce_scatter | solution.py:92
  215.6 7.3 %collective-permute-start = (bf16[32,2048]{1,0:T(8,128)(2,1)S(1)}, bf16[32,2048]{1,0:T(8,128)(2,1)S(1)}, u32[]{:S(2)}, u32[]{:S(2)}) collective-permute-start(bf16[32,2048]{1,0:T(8,128)(2,1)S(1)} %broadcast_select_fusion.2), channel_id=1, source_target_pairs={{8,0},{10,2},{12,4},{14,6},{16,8},{18,10},{20,12},{22,14},{24,16},... | collective-permute-start | bytes 393224 | tf_op jit(solution)/shard_map/while/body/eval_jaxpr/ppermute | solution.py:21
  223.0 1.4 collective-permute-start.1
  224.5 8.4 %collective-permute-start.2 = (bf16[32,4096]{1,0:T(8,128)(2,1)S(1)}, bf16[32,4096]{1,0:T(8,128)(2,1)S(1)}, u32[]{:S(2)}, u32[]{:S(2)}) collective-permute-start(bf16[32,4096]{1,0:T(8,128)(2,1)S(1)} %maximum_select_fusion.13), channel_id=1, source_target_pairs={{0,4},{2,6},{4,0},{6,2},{8,12},{10,14},{12,8},{14,10},{16,20},{18,... | collective-permute-start | bytes 786440 | tf_op jit(solution)/shard_map/while/body/eval_jaxpr/ppermute | solution.py:15
  289.2 72.6 %reduce-scatter.2.cloned.1.call-start = ((), (), s32[]{:S(2)}) async-start(), calls=%async_computation.2 | async-start | bytes 786432 | tf_op jit(solution)/shard_map/while/body/eval_jaxpr/reduce_scatter | solution.py:92
  289.3 7.3 %collective-permute-start = (bf16[32,2048]{1,0:T(8,128)(2,1)S(1)}, bf16[32,2048]{1,0:T(8,128)(2,1)S(1)}, u32[]{:S(2)}, u32[]{:S(2)}) collective-permute-start(bf16[32,2048]{1,0:T(8,128)(2,1)S(1)} %broadcast_select_fusion.2), channel_id=1, source_target_pairs={{8,0},{10,2},{12,4},{14,6},{16,8},{18,10},{20,12},{22,14},{24,16},... | collective-permute-start | bytes 393224 | tf_op jit(solution)/shard_map/while/body/eval_jaxpr/ppermute | solution.py:21
  296.7 1.4 collective-permute-start.1
  298.2 8.4 %collective-permute-start.2 = (bf16[32,4096]{1,0:T(8,128)(2,1)S(1)}, bf16[32,4096]{1,0:T(8,128)(2,1)S(1)}, u32[]{:S(2)}, u32[]{:S(2)}) collective-permute-start(bf16[32,4096]{1,0:T(8,128)(2,1)S(1)} %maximum_select_fusion.13), channel_id=1, source_target_pairs={{0,4},{2,6},{4,0},{6,2},{8,12},{10,14},{12,8},{14,10},{16,20},{18,... | collective-permute-start | bytes 786440 | tf_op jit(solution)/shard_map/while/body/eval_jaxpr/ppermute | solution.py:15
  362.9 72.6 %reduce-scatter.2.cloned.1.call-start = ((), (), s32[]{:S(2)}) async-start(), calls=%async_computation.2 | async-start | bytes 786432 | tf_op jit(solution)/shard_map/while/body/eval_jaxpr/reduce_scatter | solution.py:92
  363.0 7.3 %collective-permute-start = (bf16[32,2048]{1,0:T(8,128)(2,1)S(1)}, bf16[32,2048]{1,0:T(8,128)(2,1)S(1)}, u32[]{:S(2)}, u32[]{:S(2)}) collective-permute-start(bf16[32,2048]{1,0:T(8,128)(2,1)S(1)} %broadcast_select_fusion.2), channel_id=1, source_target_pairs={{8,0},{10,2},{12,4},{14,6},{16,8},{18,10},{20,12},{22,14},{24,16},... | collective-permute-start | bytes 393224 | tf_op jit(solution)/shard_map/while/body/eval_jaxpr/ppermute | solution.py:21
  370.4 1.4 collective-permute-start.1
  371.9 8.4 %collective-permute-start.2 = (bf16[32,4096]{1,0:T(8,128)(2,1)S(1)}, bf16[32,4096]{1,0:T(8,128)(2,1)S(1)}, u32[]{:S(2)}, u32[]{:S(2)}) collective-permute-start(bf16[32,4096]{1,0:T(8,128)(2,1)S(1)} %maximum_select_fusion.13), channel_id=1, source_target_pairs={{0,4},{2,6},{4,0},{6,2},{8,12},{10,14},{12,8},{14,10},{16,20},{18,... | collective-permute-start | bytes 786440 | tf_op jit(solution)/shard_map/while/body/eval_jaxpr/ppermute | solution.py:15
  436.6 0.7 copy-start.1
  436.6 0.7 copy-start.4
Sparse Core Ops, SparseCore 0:
  107.5 14.0 reduce-scatter.1
  181.4 10.9 reduce-scatter.1
  255.0 10.9 reduce-scatter.1
  328.7 10.9 reduce-scatter.1
  402.4 10.9 reduce-scatter.1
where the time goes:
time: 445 us; the launch traced here: 444 us
  blocking collectives  199 us (45%)
  waiting for transfers between devices  123 us (28%)
  matrix products  76.6 us (17%)
  other arithmetic  17.1 us (4%)
  between operations  13.8 us (3%)
  starting transfers between devices  12.5 us (3%)
    psum x5, blocking collectives, advance(): totals = totals + lax.psum(increment, 'section')  148 us
    ppermute x12, waiting for transfers between devices, from_partner(): return lax.ppermute(value, axis, pairs)  93.7 us
    dot_general x5, matrix products, advance(): lax.dot_general(by_group, weights, (((1,), (1,)), ((), ())), preferred_el...  58.9 us
    all_to_all x5, blocking collectives, advance(): lax.all_to_all(gate_full, 'dp', split_axis=1, concat_axis=0, tiled=True)  50.8 us
    ppermute x5, waiting for transfers between devices, from_behind(): lax.ppermute(value, axis, [(source, source + steps) for source in range(f...  28.9 us
    dot_general x5, matrix products, score_terms(): jnp.dot(gate_full, right_full, preferred_element_type=jnp.float32)  14.9 us
  transfers between devices with their start and end apart: 22, of which 17 were waited for; matrix products, arithmetic and copies ran while one was open for 5% of the time, Pallas kernels for 0%

commit v1 on v0

--- a/solution.py
+++ b/solution.py
@@ -7,6 +7,11 @@
 QUERIES = 16
 RANK = 16
 ROWS = 32
+
+
+def gather_and_add(block, axis):
+    parts = lax.all_gather(block, axis)
+    return jnp.sum(parts, axis=0)
 
 
 def from_partner(value, axis, distance):
@@ -102,7 +107,7 @@
         updated = lax.dynamic_update_slice_in_dim(grad_store, in_grad, row_start, 0)
         grad_store = jnp.where(in_range, updated, grad_store)
         increment = jnp.where(in_range, increment, 0.0)
-        totals = totals + lax.psum(increment, "section")
+        totals = totals + gather_and_add(increment, "section")
         return (in_grad, grad_store, totals)
 
     initial = (

time: 445 us -> 391 us (0.88)
  blocking collectives: 199 us -> 143 us
    psum x5 -> x0, blocking collectives: 148 us -> none  [advance(): totals = totals + lax.psum(increment, 'section')]
    all_gather x0 -> x5, blocking collectives: none -> 92.3 us  [gather_and_add(): parts = lax.all_gather(block, axis)]
where the time goes in v1:
time: 391 us; the launch traced here: 390 us
  blocking collectives  143 us (37%)
  waiting for transfers between devices  121 us (31%)
  matrix products  76.6 us (20%)
  other arithmetic  17.3 us (4%)
  starting transfers between devices  16.2 us (4%)
  between operations  13.8 us (4%)
    all_gather x5, blocking collectives, gather_and_add(): parts = lax.all_gather(block, axis)  92.3 us
    ppermute x12, waiting for transfers between devices, from_partner(): return lax.ppermute(value, axis, pairs)  90.1 us
    dot_general x5, matrix products, advance(): lax.dot_general(by_group, weights, (((1,), (1,)), ((), ())), preferred_el...  58.9 us
    all_to_all x5, blocking collectives, advance(): lax.all_to_all(gate_full, 'dp', split_axis=1, concat_axis=0, tiled=True)  50.8 us
    ppermute x5, waiting for transfers between devices, from_behind(): lax.ppermute(value, axis, [(source, source + steps) for source in range(f...  30.8 us
    dot_general x5, matrix products, score_terms(): jnp.dot(gate_full, right_full, preferred_element_type=jnp.float32)  14.9 us
    ppermute x12, starting transfers between devices, from_partner(): return lax.ppermute(value, axis, pairs)  9.51 us
    select_n x2, other arithmetic, per_device(): jnp.where(upper_half == 1, jnp.concatenate([partner, right_full], 0), jnp...  8.88 us
  transfers between devices with their start and end apart: 22, of which 17 were waited for; matrix products, arithmetic and copies ran while one was open for 5% of the time, Pallas kernels for 0%

profile of v1, /device:TPU:0, one launch (start us, length us, event | category | flops | bytes accessed | tf_op | source)
XLA Modules:
  0.0 390.2 jit_solution(15185592698765206461)
XLA Ops:
  7.2 0.6 collective-permute-start.3
  7.7 2.5 collective-permute-done.3
  10.2 3.4 maximum_select_fusion.6
  13.6 2.8 collective-permute-start.4
  16.6 1.1 multiply_convert_fusion
  17.8 44.9 %collective-permute-done.4 = bf16[4096,256]{1,0:T(8,128)(2,1)} collective-permute-done((bf16[4096,256]{1,0:T(8,128)(2,1)}, bf16[4096,256]{1,0:T(8,128)(2,1)}, u32[]{:S(2)}, u32[]{:S(2)}) %collective-permute-start.4) | collective-permute-done | bytes 2097184 | tf_op jit(solution)/shard_map/ppermute | solution.py:20
  62.7 5.5 %maximum_select_fusion.5 = bf16[8192,256]{1,0:T(8,128)(2,1)} fusion(bf16[4096,256]{1,0:T(8,128)(2,1)} %maximum_select_fusion.6, bf16[4096,256]{1,0:T(8,128)(2,1)} %collective-permute-done.4, pred[]{:T(512)} %eq.87), kind=kLoop, calls=%fused_computation.38 | loop fusion | flops 18874368 | bytes 8388609 | tf_op jit(solution)/shard_map/jit(_where)/select_n | solution.py:58
  68.3 314.7 %while.20 = (s32[]{:T(128)}, bf16[32,2048]{1,0:T(8,128)(2,1)S(1)}, bf16[64,2048]{1,0:T(8,128)(2,1)S(1)}, f32[2,16]{1,0:T(2,128)S(1)}, pred[]{:T(512)}, /*index=5...) while((s32[]{:T(128)}, bf16[32,2048]{1,0:T(8,128)(2,1)S(1)}, ...), condition=%wide.region_4.5_spmd.clone, body=%wide.region_0.4_spmd.clone.sunk | while | flops 1248227584 | bytes 33236612 | solution.py:118
  68.4 1.3 collective-permute-start
  69.7 5.5 %collective-permute-done = bf16[32,2048]{1,0:T(8,128)(2,1)S(1)} collective-permute-done((bf16[32,2048]{1,0:T(8,128)(2,1)S(1)}, bf16[32,2048]{1,0:T(8,128)(2,1)S(1)}, u32[]{:S(2)}, u32[]{:S(2)}) %collective-permute-start) | collective-permute-done | bytes 131104 | tf_op jit(solution)/shard_map/while/body/eval_jaxpr/ppermute | solution.py:26
  75.4 1.3 collective-permute-done.1
  76.8 1.8 collective-permute-start.2
  78.7 6.5 %collective-permute-done.2 = bf16[32,4096]{1,0:T(8,128)(2,1)S(1)} collective-permute-done((bf16[32,4096]{1,0:T(8,128)(2,1)S(1)}, bf16[32,4096]{1,0:T(8,128)(2,1)S(1)}, u32[]{:S(2)}, u32[]{:S(2)}) %collective-permute-start.2) | collective-permute-done | bytes 262176 | tf_op jit(solution)/shard_map/while/body/eval_jaxpr/ppermute | solution.py:20
  85.3 10.3 %all_to_all.38 = bf16[32,2,4096]{2,0,1:T(8,128)(2,1)S(1)} all-to-all(bf16[32,2,4096]{2,0,1:T(8,128)(2,1)S(1)} %maximum_select_fusion.14), channel_id=1, replica_groups=mesh['section'=16,'dp'=2] {'dp'}, dimensions={1} | all-to-all | bytes 1048576 | tf_op jit(solution)/shard_map/while/body/eval_jaxpr/all_to_all | solution.py:96
  95.6 11.8 %fusion.52 = f32[64,2048]{1,0:T(8,128)} fusion(bf16[64,4096]{1,0:T(8,128)(2,1)S(1)} %bitcast.48, bf16[2048,4096]{1,0:T(8,128)(2,1)} %get-tuple-element.581), kind=kOutput, calls=%fused_computation.50.clone.1 | convolution fusion | flops 1073741824 | bytes 17825792 | tf_op jit(solution)/shard_map/while/body/eval_jaxpr/dot_general | solution.py:98
  107.5 0.3 fusion.53
  107.8 2.9 convolution_multiply_fusion.2
  111.1 19.8 %all-gather.4 = f32[16,2,16]{2,1,0:T(2,128)S(1)} all-gather(f32[1,2,16]{2,1,0:T(2,128)S(1)} %fusion.54), channel_id=2, replica_groups=mesh['section'=16,'dp'=2] {'section'}, dimensions={0}, use_global_device_ids=true | all-gather | bytes 2176 | tf_op jit(solution)/shard_map/while/body/eval_jaxpr/all_gather | solution.py:13
  130.9 1.0 select_dynamic-update-slice_fusion.2
  132.1 1.3 collective-permute-start
  133.4 6.3 %collective-permute-done = bf16[32,2048]{1,0:T(8,128)(2,1)S(1)} collective-permute-done((bf16[32,2048]{1,0:T(8,128)(2,1)S(1)}, bf16[32,2048]{1,0:T(8,128)(2,1)S(1)}, u32[]{:S(2)}, u32[]{:S(2)}) %collective-permute-start) | collective-permute-done | bytes 131104 | tf_op jit(solution)/shard_map/while/body/eval_jaxpr/ppermute | solution.py:26
  139.9 1.3 collective-permute-done.1
  141.5 8.3 %collective-permute-done.2 = bf16[32,4096]{1,0:T(8,128)(2,1)S(1)} collective-permute-done((bf16[32,4096]{1,0:T(8,128)(2,1)S(1)}, bf16[32,4096]{1,0:T(8,128)(2,1)S(1)}, u32[]{:S(2)}, u32[]{:S(2)}) %collective-permute-start.2) | collective-permute-done | bytes 262176 | tf_op jit(solution)/shard_map/while/body/eval_jaxpr/ppermute | solution.py:20
  149.8 10.1 %all_to_all.38 = bf16[32,2,4096]{2,0,1:T(8,128)(2,1)S(1)} all-to-all(bf16[32,2,4096]{2,0,1:T(8,128)(2,1)S(1)} %maximum_select_fusion.14), channel_id=1, replica_groups=mesh['section'=16,'dp'=2] {'dp'}, dimensions={1} | all-to-all | bytes 1048576 | tf_op jit(solution)/shard_map/while/body/eval_jaxpr/all_to_all | solution.py:96
  159.9 11.8 %fusion.52 = f32[64,2048]{1,0:T(8,128)} fusion(bf16[64,4096]{1,0:T(8,128)(2,1)S(1)} %bitcast.48, bf16[2048,4096]{1,0:T(8,128)(2,1)} %get-tuple-element.581), kind=kOutput, calls=%fused_computation.50.clone.1 | convolution fusion | flops 1073741824 | bytes 17825792 | tf_op jit(solution)/shard_map/while/body/eval_jaxpr/dot_general | solution.py:98
  171.8 0.3 fusion.53
  172.1 3.0 convolution_multiply_fusion.2
  175.5 17.6 %all-gather.4 = f32[16,2,16]{2,1,0:T(2,128)S(1)} all-gather(f32[1,2,16]{2,1,0:T(2,128)S(1)} %fusion.54), channel_id=2, replica_groups=mesh['section'=16,'dp'=2] {'section'}, dimensions={0}, use_global_device_ids=true | all-gather | bytes 2176 | tf_op jit(solution)/shard_map/while/body/eval_jaxpr/all_gather | solution.py:13
  193.2 1.0 select_dynamic-update-slice_fusion.2
  194.3 1.3 collective-permute-start
  195.6 6.3 %collective-permute-done = bf16[32,2048]{1,0:T(8,128)(2,1)S(1)} collective-permute-done((bf16[32,2048]{1,0:T(8,128)(2,1)S(1)}, bf16[32,2048]{1,0:T(8,128)(2,1)S(1)}, u32[]{:S(2)}, u32[]{:S(2)}) %collective-permute-start) | collective-permute-done | bytes 131104 | tf_op jit(solution)/shard_map/while/body/eval_jaxpr/ppermute | solution.py:26
  202.1 1.3 collective-permute-done.1
  203.6 1.6 collective-permute-start.2
  205.2 6.7 %collective-permute-done.2 = bf16[32,4096]{1,0:T(8,128)(2,1)S(1)} collective-permute-done((bf16[32,4096]{1,0:T(8,128)(2,1)S(1)}, bf16[32,4096]{1,0:T(8,128)(2,1)S(1)}, u32[]{:S(2)}, u32[]{:S(2)}) %collective-permute-start.2) | collective-permute-done | bytes 262176 | tf_op jit(solution)/shard_map/while/body/eval_jaxpr/ppermute | solution.py:20
  212.1 10.1 %all_to_all.38 = bf16[32,2,4096]{2,0,1:T(8,128)(2,1)S(1)} all-to-all(bf16[32,2,4096]{2,0,1:T(8,128)(2,1)S(1)} %maximum_select_fusion.14), channel_id=1, replica_groups=mesh['section'=16,'dp'=2] {'dp'}, dimensions={1} | all-to-all | bytes 1048576 | tf_op jit(solution)/shard_map/while/body/eval_jaxpr/all_to_all | solution.py:96
  222.2 11.8 %fusion.52 = f32[64,2048]{1,0:T(8,128)} fusion(bf16[64,4096]{1,0:T(8,128)(2,1)S(1)} %bitcast.48, bf16[2048,4096]{1,0:T(8,128)(2,1)} %get-tuple-element.581), kind=kOutput, calls=%fused_computation.50.clone.1 | convolution fusion | flops 1073741824 | bytes 17825792 | tf_op jit(solution)/shard_map/while/body/eval_jaxpr/dot_general | solution.py:98
  234.1 0.3 fusion.53
  234.4 2.9 convolution_multiply_fusion.2
  237.4 0.3 fusion.54
  237.7 18.7 %all-gather.4 = f32[16,2,16]{2,1,0:T(2,128)S(1)} all-gather(f32[1,2,16]{2,1,0:T(2,128)S(1)} %fusion.54), channel_id=2, replica_groups=mesh['section'=16,'dp'=2] {'section'}, dimensions={0}, use_global_device_ids=true | all-gather | bytes 2176 | tf_op jit(solution)/shard_map/while/body/eval_jaxpr/all_gather | solution.py:13
  256.4 1.0 select_dynamic-update-slice_fusion.2
  257.5 1.3 collective-permute-start
  258.8 6.3 %collective-permute-done = bf16[32,2048]{1,0:T(8,128)(2,1)S(1)} collective-permute-done((bf16[32,2048]{1,0:T(8,128)(2,1)S(1)}, bf16[32,2048]{1,0:T(8,128)(2,1)S(1)}, u32[]{:S(2)}, u32[]{:S(2)}) %collective-permute-start) | collective-permute-done | bytes 131104 | tf_op jit(solution)/shard_map/while/body/eval_jaxpr/ppermute | solution.py:26
  265.4 1.3 collective-permute-done.1
  266.8 0.6 collective-permute-start.2
  267.4 7.8 %collective-permute-done.2 = bf16[32,4096]{1,0:T(8,128)(2,1)S(1)} collective-permute-done((bf16[32,4096]{1,0:T(8,128)(2,1)S(1)}, bf16[32,4096]{1,0:T(8,128)(2,1)S(1)}, u32[]{:S(2)}, u32[]{:S(2)}) %collective-permute-start.2) | collective-permute-done | bytes 262176 | tf_op jit(solution)/shard_map/while/body/eval_jaxpr/ppermute | solution.py:20
  275.3 10.1 %all_to_all.38 = bf16[32,2,4096]{2,0,1:T(8,128)(2,1)S(1)} all-to-all(bf16[32,2,4096]{2,0,1:T(8,128)(2,1)S(1)} %maximum_select_fusion.14), channel_id=1, replica_groups=mesh['section'=16,'dp'=2] {'dp'}, dimensions={1} | all-to-all | bytes 1048576 | tf_op jit(solution)/shard_map/while/body/eval_jaxpr/all_to_all | solution.py:96
  285.4 11.8 %fusion.52 = f32[64,2048]{1,0:T(8,128)} fusion(bf16[64,4096]{1,0:T(8,128)(2,1)S(1)} %bitcast.48, bf16[2048,4096]{1,0:T(8,128)(2,1)} %get-tuple-element.581), kind=kOutput, calls=%fused_computation.50.clone.1 | convolution fusion | flops 1073741824 | bytes 17825792 | tf_op jit(solution)/shard_map/while/body/eval_jaxpr/dot_general | solution.py:98
  297.3 0.3 fusion.53
  297.6 3.0 convolution_multiply_fusion.2
  301.0 17.5 %all-gather.4 = f32[16,2,16]{2,1,0:T(2,128)S(1)} all-gather(f32[1,2,16]{2,1,0:T(2,128)S(1)} %fusion.54), channel_id=2, replica_groups=mesh['section'=16,'dp'=2] {'section'}, dimensions={0}, use_global_device_ids=true | all-gather | bytes 2176 | tf_op jit(solution)/shard_map/while/body/eval_jaxpr/all_gather | solution.py:13
  318.6 1.0 select_dynamic-update-slice_fusion.2
  319.7 1.3 collective-permute-start
  321.0 6.3 %collective-permute-done = bf16[32,2048]{1,0:T(8,128)(2,1)S(1)} collective-permute-done((bf16[32,2048]{1,0:T(8,128)(2,1)S(1)}, bf16[32,2048]{1,0:T(8,128)(2,1)S(1)}, u32[]{:S(2)}, u32[]{:S(2)}) %collective-permute-start) | collective-permute-done | bytes 131104 | tf_op jit(solution)/shard_map/while/body/eval_jaxpr/ppermute | solution.py:26
  327.5 1.3 collective-permute-done.1
  329.0 1.7 collective-permute-start.2
  330.7 6.6 %collective-permute-done.2 = bf16[32,4096]{1,0:T(8,128)(2,1)S(1)} collective-permute-done((bf16[32,4096]{1,0:T(8,128)(2,1)S(1)}, bf16[32,4096]{1,0:T(8,128)(2,1)S(1)}, u32[]{:S(2)}, u32[]{:S(2)}) %collective-permute-start.2) | collective-permute-done | bytes 262176 | tf_op jit(solution)/shard_map/while/body/eval_jaxpr/ppermute | solution.py:20
  337.5 10.1 %all_to_all.38 = bf16[32,2,4096]{2,0,1:T(8,128)(2,1)S(1)} all-to-all(bf16[32,2,4096]{2,0,1:T(8,128)(2,1)S(1)} %maximum_select_fusion.14), channel_id=1, replica_groups=mesh['section'=16,'dp'=2] {'dp'}, dimensions={1} | all-to-all | bytes 1048576 | tf_op jit(solution)/shard_map/while/body/eval_jaxpr/all_to_all | solution.py:96
  347.6 11.8 %fusion.52 = f32[64,2048]{1,0:T(8,128)} fusion(bf16[64,4096]{1,0:T(8,128)(2,1)S(1)} %bitcast.48, bf16[2048,4096]{1,0:T(8,128)(2,1)} %get-tuple-element.581), kind=kOutput, calls=%fused_computation.50.clone.1 | convolution fusion | flops 1073741824 | bytes 17825792 | tf_op jit(solution)/shard_map/while/body/eval_jaxpr/dot_general | solution.py:98
  359.5 0.3 fusion.53
  359.8 2.9 convolution_multiply_fusion.2
  363.1 18.8 %all-gather.4 = f32[16,2,16]{2,1,0:T(2,128)S(1)} all-gather(f32[1,2,16]{2,1,0:T(2,128)S(1)} %fusion.54), channel_id=2, replica_groups=mesh['section'=16,'dp'=2] {'section'}, dimensions={0}, use_global_device_ids=true | all-gather | bytes 2176 | tf_op jit(solution)/shard_map/while/body/eval_jaxpr/all_gather | solution.py:13
  381.9 1.0 select_dynamic-update-slice_fusion.2
  383.0 0.7 copy-done.1
  (98 shorter events, 5.1 us)
Async XLA Ops:
  7.2 9.3 %copy-start.5 = (s32[2]{0:T(128)S(1)}, s32[2]{0:T(128)}, u32[]{:S(2)}) copy-start(s32[2]{0:T(128)} %param.11) | copy-start | bytes 28
  7.2 9.3 %copy-start.6 = (s32[64]{0:T(128)S(1)}, s32[64]{0:T(128)}, u32[]{:S(2)}) copy-start(s32[64]{0:T(128)} %param.12) | copy-start | bytes 772
  7.2 3.1 collective-permute-start.3
  13.6 49.1 %collective-permute-start.4 = (bf16[4096,256]{1,0:T(8,128)(2,1)}, bf16[4096,256]{1,0:T(8,128)(2,1)}, u32[]{:S(2)}, u32[]{:S(2)}) collective-permute-start(bf16[4096,256]{1,0:T(8,128)(2,1)} %maximum_select_fusion.6), channel_id=1, source_target_pairs={{0,4},{2,6},{4,0},{6,2},{8,12},{10,14},{12,8},{14,10},{16,20},{18,... | collective-permute-start | bytes 6291464 | tf_op jit(solution)/shard_map/ppermute | solution.py:20
  17.8 50.5 %copy-start = (bf16[2048,256]{1,0:T(8,128)(2,1)S(1)}, bf16[2048,256]{1,0:T(8,128)(2,1)}, u32[]{:S(2)}) copy-start(bf16[2048,256]{1,0:T(8,128)(2,1)} %param.16) | copy-start | bytes 3145732
  17.8 50.5 %copy-start.2 = (bf16[64,2048]{1,0:T(8,128)(2,1)S(1)}, bf16[64,2048]{1,0:T(8,128)(2,1)}, u32[]{:S(2)}) copy-start(bf16[64,2048]{1,0:T(8,128)(2,1)} %param.13) | copy-start | bytes 786436
  17.8 50.5 %copy-start.3 = (bf16[64,2048]{1,0:T(8,128)(2,1)S(1)}, bf16[64,2048]{1,0:T(8,128)(2,1)}, u32[]{:S(2)}) copy-start(bf16[64,2048]{1,0:T(8,128)(2,1)} %param.14) | copy-start | bytes 786436
  68.3 62.6 %reduce-scatter.2.cloned.1.call-start = ((), (), s32[]{:S(2)}) async-start(), calls=%async_computation.2 | async-start | bytes 786432 | tf_op jit(solution)/shard_map/while/body/eval_jaxpr/reduce_scatter | solution.py:97
  68.4 6.9 %collective-permute-start = (bf16[32,2048]{1,0:T(8,128)(2,1)S(1)}, bf16[32,2048]{1,0:T(8,128)(2,1)S(1)}, u32[]{:S(2)}, u32[]{:S(2)}) collective-permute-start(bf16[32,2048]{1,0:T(8,128)(2,1)S(1)} %broadcast_select_fusion.2), channel_id=1, source_target_pairs={{8,0},{10,2},{12,4},{14,6},{16,8},{18,10},{20,12},{22,14},{24,16},... | collective-permute-start | bytes 393224 | tf_op jit(solution)/shard_map/while/body/eval_jaxpr/ppermute | solution.py:26
  75.3 1.4 collective-permute-start.1
  76.8 8.4 %collective-permute-start.2 = (bf16[32,4096]{1,0:T(8,128)(2,1)S(1)}, bf16[32,4096]{1,0:T(8,128)(2,1)S(1)}, u32[]{:S(2)}, u32[]{:S(2)}) collective-permute-start(bf16[32,4096]{1,0:T(8,128)(2,1)S(1)} %maximum_select_fusion.13), channel_id=1, source_target_pairs={{0,4},{2,6},{4,0},{6,2},{8,12},{10,14},{12,8},{14,10},{16,20},{18,... | collective-permute-start | bytes 786440 | tf_op jit(solution)/shard_map/while/body/eval_jaxpr/ppermute | solution.py:20
  132.0 61.2 %reduce-scatter.2.cloned.1.call-start = ((), (), s32[]{:S(2)}) async-start(), calls=%async_computation.2 | async-start | bytes 786432 | tf_op jit(solution)/shard_map/while/body/eval_jaxpr/reduce_scatter | solution.py:97
  132.1 7.6 %collective-permute-start = (bf16[32,2048]{1,0:T(8,128)(2,1)S(1)}, bf16[32,2048]{1,0:T(8,128)(2,1)S(1)}, u32[]{:S(2)}, u32[]{:S(2)}) collective-permute-start(bf16[32,2048]{1,0:T(8,128)(2,1)S(1)} %broadcast_select_fusion.2), channel_id=1, source_target_pairs={{8,0},{10,2},{12,4},{14,6},{16,8},{18,10},{20,12},{22,14},{24,16},... | collective-permute-start | bytes 393224 | tf_op jit(solution)/shard_map/while/body/eval_jaxpr/ppermute | solution.py:26
  139.8 1.4 collective-permute-start.1
  141.3 8.4 %collective-permute-start.2 = (bf16[32,4096]{1,0:T(8,128)(2,1)S(1)}, bf16[32,4096]{1,0:T(8,128)(2,1)S(1)}, u32[]{:S(2)}, u32[]{:S(2)}) collective-permute-start(bf16[32,4096]{1,0:T(8,128)(2,1)S(1)} %maximum_select_fusion.13), channel_id=1, source_target_pairs={{0,4},{2,6},{4,0},{6,2},{8,12},{10,14},{12,8},{14,10},{16,20},{18,... | collective-permute-start | bytes 786440 | tf_op jit(solution)/shard_map/while/body/eval_jaxpr/ppermute | solution.py:20
  194.2 62.2 %reduce-scatter.2.cloned.1.call-start = ((), (), s32[]{:S(2)}) async-start(), calls=%async_computation.2 | async-start | bytes 786432 | tf_op jit(solution)/shard_map/while/body/eval_jaxpr/reduce_scatter | solution.py:97
  194.3 7.6 %collective-permute-start = (bf16[32,2048]{1,0:T(8,128)(2,1)S(1)}, bf16[32,2048]{1,0:T(8,128)(2,1)S(1)}, u32[]{:S(2)}, u32[]{:S(2)}) collective-permute-start(bf16[32,2048]{1,0:T(8,128)(2,1)S(1)} %broadcast_select_fusion.2), channel_id=1, source_target_pairs={{8,0},{10,2},{12,4},{14,6},{16,8},{18,10},{20,12},{22,14},{24,16},... | collective-permute-start | bytes 393224 | tf_op jit(solution)/shard_map/while/body/eval_jaxpr/ppermute | solution.py:26
  202.1 1.4 collective-permute-start.1
  203.6 8.4 %collective-permute-start.2 = (bf16[32,4096]{1,0:T(8,128)(2,1)S(1)}, bf16[32,4096]{1,0:T(8,128)(2,1)S(1)}, u32[]{:S(2)}, u32[]{:S(2)}) collective-permute-start(bf16[32,4096]{1,0:T(8,128)(2,1)S(1)} %maximum_select_fusion.13), channel_id=1, source_target_pairs={{0,4},{2,6},{4,0},{6,2},{8,12},{10,14},{12,8},{14,10},{16,20},{18,... | collective-permute-start | bytes 786440 | tf_op jit(solution)/shard_map/while/body/eval_jaxpr/ppermute | solution.py:20
  257.4 61.1 %reduce-scatter.2.cloned.1.call-start = ((), (), s32[]{:S(2)}) async-start(), calls=%async_computation.2 | async-start | bytes 786432 | tf_op jit(solution)/shard_map/while/body/eval_jaxpr/reduce_scatter | solution.py:97
  257.5 7.6 %collective-permute-start = (bf16[32,2048]{1,0:T(8,128)(2,1)S(1)}, bf16[32,2048]{1,0:T(8,128)(2,1)S(1)}, u32[]{:S(2)}, u32[]{:S(2)}) collective-permute-start(bf16[32,2048]{1,0:T(8,128)(2,1)S(1)} %broadcast_select_fusion.2), channel_id=1, source_target_pairs={{8,0},{10,2},{12,4},{14,6},{16,8},{18,10},{20,12},{22,14},{24,16},... | collective-permute-start | bytes 393224 | tf_op jit(solution)/shard_map/while/body/eval_jaxpr/ppermute | solution.py:26
  265.3 1.4 collective-permute-start.1
  266.8 8.4 %collective-permute-start.2 = (bf16[32,4096]{1,0:T(8,128)(2,1)S(1)}, bf16[32,4096]{1,0:T(8,128)(2,1)S(1)}, u32[]{:S(2)}, u32[]{:S(2)}) collective-permute-start(bf16[32,4096]{1,0:T(8,128)(2,1)S(1)} %maximum_select_fusion.13), channel_id=1, source_target_pairs={{0,4},{2,6},{4,0},{6,2},{8,12},{10,14},{12,8},{14,10},{16,20},{18,... | collective-permute-start | bytes 786440 | tf_op jit(solution)/shard_map/while/body/eval_jaxpr/ppermute | solution.py:20
  319.6 62.3 %reduce-scatter.2.cloned.1.call-start = ((), (), s32[]{:S(2)}) async-start(), calls=%async_computation.2 | async-start | bytes 786432 | tf_op jit(solution)/shard_map/while/body/eval_jaxpr/reduce_scatter | solution.py:97
  319.7 7.6 %collective-permute-start = (bf16[32,2048]{1,0:T(8,128)(2,1)S(1)}, bf16[32,2048]{1,0:T(8,128)(2,1)S(1)}, u32[]{:S(2)}, u32[]{:S(2)}) collective-permute-start(bf16[32,2048]{1,0:T(8,128)(2,1)S(1)} %broadcast_select_fusion.2), channel_id=1, source_target_pairs={{8,0},{10,2},{12,4},{14,6},{16,8},{18,10},{20,12},{22,14},{24,16},... | collective-permute-start | bytes 393224 | tf_op jit(solution)/shard_map/while/body/eval_jaxpr/ppermute | solution.py:26
  327.5 1.4 collective-permute-start.1
  329.0 8.4 %collective-permute-start.2 = (bf16[32,4096]{1,0:T(8,128)(2,1)S(1)}, bf16[32,4096]{1,0:T(8,128)(2,1)S(1)}, u32[]{:S(2)}, u32[]{:S(2)}) collective-permute-start(bf16[32,4096]{1,0:T(8,128)(2,1)S(1)} %maximum_select_fusion.13), channel_id=1, source_target_pairs={{0,4},{2,6},{4,0},{6,2},{8,12},{10,14},{12,8},{14,10},{16,20},{18,... | collective-permute-start | bytes 786440 | tf_op jit(solution)/shard_map/while/body/eval_jaxpr/ppermute | solution.py:20
  383.0 0.7 copy-start.1
  383.0 0.7 copy-start.4
Sparse Core Ops, SparseCore 0:
  107.5 14.0 reduce-scatter.1
  171.9 10.9 reduce-scatter.1
  234.1 11.9 reduce-scatter.1
  297.3 10.8 reduce-scatter.1
  359.5 12.0 reduce-scatter.1
